TPU v7x, 32 devices: a whole 2x2x4 slice. The times are simulated.
32 devices in a mesh: groups: 1, ep: 32 (over z, y, x, core).
Axes of the slice: x: 2, y: 2, z: 4, core: 2. Of those that a mesh axis runs over, the one named last changes fastest.
Arguments:
- tokens: bfloat16 [2048, 2880], P(('groups', 'ep')), may hold values from -6 to 6
- routes: int32 [2048, 4], P(('groups', 'ep')), may hold values from 0 to 7, all different within a row; in each aligned block of 64 rows (0 to 63, 64 to 127, ...) at most 36 rows name the same one
- norm_gain: bfloat16 [2880], replicated, may hold values from 0.25 to 1.75
- router_weight: bfloat16 [2880, 8], replicated, may hold values from -0.02734375 to 0.02734375
- gate_up_weight: bfloat16 [32, 2880, 720], P('ep'), may hold values from -0.109375 to 0.109375
- down_weight: bfloat16 [32, 360, 2880], P('ep'), may hold values from -0.15625 to 0.15625
Outputs:
- mixed: bfloat16 [2048, 2880], P(('groups', 'ep'))
Inputs may be any that keep to these rules, and one draw needn't show every extreme that they name: `routes`: in each aligned block of 64 rows (the rows of one device), no expert is named by more than 36 rows; in some blocks one expert is named by exactly 36 rows. A row names 4 different experts.
All inputs are finite; a program needn't handle non-finite values.
Results may differ from a plain program's by a relative error of at most 0.005.
Values may be sent and summed in bfloat16 or wider, within the bound.
A program may use at most 128 MiB of HBM per device.

v0:
```python
import functools

import jax
import jax.numpy as jnp
from jax import lax
from jax.experimental import pallas as pl
from jax.experimental.pallas import tpu as pltpu
from jax.sharding import PartitionSpec as P

SHARD = 4
MESH = pl.DeviceIdType.MESH


def places(groups):
    me = lax.axis_index("ep")
    group = me // SHARD
    member = me % SHARD
    core = member % 2
    half = member // 2
    core_mate = me + 1 - 2 * core
    chip_mate = me + 2 - 4 * half
    return me, group, member, core, half, core_mate, chip_mate


def greet(groups, group, member, core_mate, chip_mate):
    barrier = pltpu.get_barrier_semaphore()
    others = [(group + r) % groups * SHARD + member for r in range(1, groups)]
    for other in [core_mate, chip_mate] + others:
        pl.semaphore_signal(barrier, inc=1, device_id={"ep": other}, device_id_type=MESH)
    pl.semaphore_wait(barrier, groups + 1)


def send(src, dst, sems, slot, device):
    return pltpu.make_async_remote_copy(
        src_ref=src,
        dst_ref=dst,
        send_sem=sems.at[0, slot],
        recv_sem=sems.at[1, slot],
        device_id={"ep": device},
        device_id_type=MESH,
    )


def far_first(groups):
    return sorted(range(groups), key=lambda r: -min(r, groups - r))


def dispatch_kernel(groups, buf, out, direct, across, paired, relayed, local):
    me, group, member, core, half, core_mate, chip_mate = places(groups)
    greet(groups, group, member, core_mate, chip_mate)
    own = pltpu.make_async_copy(buf.at[group], out.at[me], local)
    own.start()
    to_chip = [send(buf.at[group], out.at[me], across, 0, chip_mate)]
    to_chip[0].start()
    turns = [1, groups - 1] + [r for r in far_first(groups) if 1 < r < groups - 1]
    sent = []
    for r in turns:
        target = (group + r) % groups
        copy = send(buf.at[target], out.at[me], direct, r, target * SHARD + member)
        copy.start()
        sent.append(copy)
    to_core = [send(buf.at[group], out.at[me], paired, 0, core_mate)]
    to_core[0].start()
    for at, r in enumerate(turns):
        source = (group + groups - r) % groups
        block = out.at[source * SHARD + member]
        sent[at].wait_recv()
        for copies, sems, device in ((to_chip, across, chip_mate), (to_core, paired, core_mate)):
            copy = send(block, block, sems, r, device)
            copy.start()
            copies.append(copy)
    relays = []
    for at, r in enumerate([0] + turns):
        source = (group + groups - r) % groups
        block = out.at[source * SHARD + (member + 2) % SHARD]
        to_chip[at].wait_recv()
        copy = send(block, block, relayed, r, core_mate)
        copy.start()
        relays.append(copy)
    for r in range(groups):
        to_core[r].wait_recv()
        relays[r].wait_recv()
    own.wait()
    for copy in sent + to_chip + to_core + relays:
        copy.wait_send()


def dispatch(buffer, devices):
    groups, rows, width = buffer.shape
    sems = pltpu.SemaphoreType.DMA((2, groups))
    return pl.pallas_call(
        functools.partial(dispatch_kernel, groups),
        out_shape=jax.ShapeDtypeStruct((devices, rows, width), buffer.dtype),
        in_specs=[pl.BlockSpec(memory_space=pltpu.VMEM)],
        out_specs=pl.BlockSpec(memory_space=pl.ANY),
        scratch_shapes=[sems, sems, sems, sems, pltpu.SemaphoreType.DMA],
        compiler_params=pltpu.CompilerParams(collective_id=0, has_side_effects=True),
    )(buffer)


def collect_kernel(
    groups, act, weight, out, part, got, summed, crossed, final, to_mate, to_chip, to_owner, local
):
    me, group, member, core, half, core_mate, chip_mate = places(groups)
    greet(groups, group, member, core_mate, chip_mate)
    rows = out.shape[1]
    chunk = SHARD * rows
    away = far_first(groups)
    owners = [(group + r) % groups for r in away]
    pairs = [
        [
            send(
                part.at[i, (half + 1 + side) % 2 * 2 + 1 - core],
                got.at[2 * i + side],
                to_mate,
                2 * i + side,
                core_mate,
            )
            for side in range(2)
        ]
        for i in range(groups)
    ]
    crossing = [send(summed.at[i], crossed.at[i], to_chip, i, chip_mate) for i in range(groups)]

    def mate_sum(i, side):
        pairs[i][side].wait_recv()
        mine = part[i, (half + 1 + side) % 2 * 2 + core].astype(jnp.float32)
        return (mine + got[2 * i + side].astype(jnp.float32)).astype(summed.dtype)

    for step in range(groups + 2):
        if step < groups:
            base = pl.multiple_of(owners[step] * chunk, chunk)
            value = jnp.dot(
                act[pl.ds(base, chunk), :], weight[...], preferred_element_type=jnp.float32
            )
            for j in range(SHARD):
                part[step, j] = value[j * rows : (j + 1) * rows].astype(part.dtype)
        if 1 <= step <= groups:
            for side in range(2):
                pairs[step - 1][side].start()
        if step >= 2:
            summed[step - 2] = mate_sum(step - 2, 0)
            final[step - 2] = mate_sum(step - 2, 1)
            crossing[step - 2].start()
    homing = [
        send(final.at[i], out.at[group], to_owner, away[i], owners[i] * SHARD + member)
        for i in range(groups - 1)
    ]
    own = pltpu.make_async_copy(final.at[groups - 1], out.at[group], local)
    for i in range(groups):
        crossing[i].wait_recv()
        total = final[i].astype(jnp.float32) + crossed[i].astype(jnp.float32)
        final[i] = total.astype(final.dtype)
        if i < groups - 1:
            homing[i].start()
        else:
            own.start()
    for copy in homing:
        copy.wait_recv()
    own.wait()
    for copy in [c for pair in pairs for c in pair] + crossing + homing:
        copy.wait_send()


def collect(activated, weight, groups, devices):
    rows = activated.shape[0] // devices
    width = weight.shape[1]
    dtype = weight.dtype
    return pl.pallas_call(
        functools.partial(collect_kernel, groups),
        out_shape=jax.ShapeDtypeStruct((groups, rows, width), dtype),
        in_specs=[pl.BlockSpec(memory_space=pltpu.VMEM)] * 2,
        out_specs=pl.BlockSpec(memory_space=pl.ANY),
        scratch_shapes=[
            pltpu.VMEM((groups, SHARD, rows, width), dtype),
            pltpu.VMEM((2 * groups, rows, width), dtype),
            pltpu.VMEM((groups, rows, width), dtype),
            pltpu.VMEM((groups, rows, width), dtype),
            pltpu.VMEM((groups, rows, width), dtype),
            pltpu.SemaphoreType.DMA((2, 2 * groups)),
            pltpu.SemaphoreType.DMA((2, groups)),
            pltpu.SemaphoreType.DMA((2, groups)),
            pltpu.SemaphoreType.DMA,
        ],
        compiler_params=pltpu.CompilerParams(
            collective_id=1, has_side_effects=True, vmem_limit_bytes=60 * 1024 * 1024
        ),
    )(activated, weight)


def shards(tokens, routes, norm_gain, router_weight, gate_up_weight, down_weight):
    tok_rows, width = tokens.shape
    top_count = routes.shape[1]
    experts = router_weight.shape[1]
    devices = lax.axis_size("ep")
    ff_dev = down_weight.shape[1]
    capacity = min(tok_rows, SHARD * (17 * tok_rows * top_count // (16 * experts * SHARD) + 1))
    capacity = -(-capacity // 8) * 8
    stream = tokens.astype(jnp.float32)
    mean_square = jnp.mean(stream * stream, axis=-1, keepdims=True)
    normed = (stream * lax.rsqrt(mean_square + 1e-05) * norm_gain.astype(jnp.float32)).astype(
        jnp.bfloat16
    )
    logits = jnp.dot(normed, router_weight, preferred_element_type=jnp.float32)
    expert_ids = lax.broadcasted_iota(jnp.int32, (1, 1, experts), 2)
    hits = jnp.any(routes[:, :, None] == expert_ids, axis=1)
    expo = jnp.where(hits, jnp.exp(logits), jnp.float32(0.0))
    prob = expo / jnp.sum(expo, axis=-1, keepdims=True)
    earlier = lax.broadcasted_iota(jnp.int32, (tok_rows, tok_rows), 1) < (
        lax.broadcasted_iota(jnp.int32, (tok_rows, tok_rows), 0)
    )
    rank = jnp.dot(
        earlier.astype(jnp.bfloat16),
        hits.astype(jnp.bfloat16),
        preferred_element_type=jnp.float32,
    ).astype(jnp.int32)
    slot = lax.broadcasted_iota(jnp.int32, (1, 1, capacity), 2)
    placed = (hits[:, :, None] & (rank[:, :, None] == slot)).reshape(tok_rows, experts * capacity)
    buffer = lax.dot_general(
        placed.astype(jnp.bfloat16),
        normed,
        (((0,), (0,)), ((), ())),
        preferred_element_type=jnp.float32,
    ).astype(jnp.bfloat16)
    received = dispatch(buffer.reshape(experts, capacity, width), devices)
    rows_in = received.reshape(devices * capacity, width)
    hidden = jnp.dot(rows_in, gate_up_weight[0], preferred_element_type=jnp.float32)
    gate_part = hidden[:, :ff_dev]
    up_part = hidden[:, ff_dev:]
    activated = ((up_part + 1.0) * gate_part * jax.nn.sigmoid(1.702 * gate_part)).astype(
        jnp.bfloat16
    )
    expert_sum = collect(activated, down_weight[0], experts, devices)
    expert_sum = expert_sum.reshape(experts * capacity, width)
    spread = jnp.repeat(prob, capacity, axis=1) * placed.astype(jnp.float32)
    high = spread.astype(jnp.bfloat16)
    low = (spread - high.astype(jnp.float32)).astype(jnp.bfloat16)
    mixture = jnp.dot(high, expert_sum, preferred_element_type=jnp.float32) + jnp.dot(
        low, expert_sum, preferred_element_type=jnp.float32
    )
    return (stream + mixture).astype(jnp.bfloat16)


def solution(mesh):
    in_specs = (
        P(("groups", "ep"), None),
        P(("groups", "ep"), None),
        P(),
        P(),
        P("ep", None, None),
        P("ep", None, None),
    )
    out_specs = P(("groups", "ep"), None)
    return jax.shard_map(shards, mesh=mesh, in_specs=in_specs, out_specs=out_specs, check_vma=False)
```

profile of v0, /device:TPU:0, one launch (start us, length us, event | category | flops | bytes accessed | tf_op | source)
XLA Modules:
  0.0 146.6 jit_solution(18328380361970656485)
XLA Ops:
  0.0 0.0 copy-start
  0.0 1.2 fusion.9
  1.2 0.7 fusion.26
  1.9 0.1 convolution_convert_fusion.1
  2.0 0.1 eq.47
  2.1 0.7 convert_element_type.40
  2.8 0.0 copy-done
  2.8 1.3 fusion.29
  4.1 0.1 fusion.14
  4.2 3.0 %convolution_convert_fusion = bf16[320,2880]{1,0:T(8,128)(2,1)} fusion(pred[64,320]{0,1:T(32,128)(4,1)S(1)} %fusion.14, bf16[64,2880]{1,0:T(8,128)(2,1)} %param.6, f32[2880]{0:T(1024)S(1)} %convert_element_type.40, f32[64]{0:T(128)S(1)} %add_rsqrt_fusion), kind=kOutput, calls=%fused_computation.2 | convolution fusion | flops 119623680 | bytes 2244096 | tf_op jit(solution)/shard_map/dot_general | solution.py:219
  7.3 68.7 %shard_map.64 = bf16[32,40,2880]{2,1,0:T(8,128)(2,1)} custom-call(bf16[8,40,2880]{2,1,0:T(8,128)(2,1)} %bitcast.29), custom_call_target="tpu_custom_call" | custom-call | tf_op jit(solution)/shard_map/pallas_call | solution.py:91
  76.0 9.9 %fusion = f32[1280,720]{1,0:T(8,128)S(1)} fusion(bf16[1280,2880]{1,0:T(8,128)(2,1)} %bitcast.28, bf16[1,2880,720]{1,2,0:T(8,128)(2,1)} %param.10), kind=kOutput, calls=%fused_computation | convolution fusion | flops 5308416000 | bytes 15206400 | tf_op jit(solution)/shard_map/dot_general | solution.py:227
  85.9 1.7 %fusion.7.act = bf16[1280,360]{1,0:T(8,128)(2,1)} fusion(f32[1280,720]{1,0:T(8,128)S(1)} %fusion), kind=kLoop, calls=%fused_computation.11 | loop fusion | flops 3686400 | bytes 4608000 | tf_op jit(solution)/shard_map/convert_element_type | solution.py:230
  87.6 55.6 %shard_map.65 = bf16[8,40,2880]{2,1,0:T(8,128)(2,1)} custom-call(bf16[1280,360]{1,0:T(8,128)(2,1)} %fusion.7.act, bf16[360,2880]{1,0:T(8,128)(2,1)} %bitcast.30), custom_call_target="tpu_custom_call" | custom-call | tf_op jit(solution)/shard_map/pallas_call | solution.py:169
  143.1 0.0 copy-start.1
  143.1 0.0 copy-start.2
  143.1 2.2 %convolution_bitcast_fusion.1 = f32[64,2880]{1,0:T(8,128)S(1)} fusion(bf16[8,40,2880]{2,1,0:T(8,128)(2,1)} %shard_map.65, f32[64,8]{0,1:T(8,128)S(1)} %broadcast_divide_fusion, s32[64,8]{0,1:T(8,128)S(1)} %convolution_convert_fusion.1, pred[64,8]{0,1:T(8,128)(4,1)S(1)} %fusion.26), kind=kOutput, calls=%fused_computation.6 | convolution fusion | flops 118026240 | bytes 2585088 | tf_op jit(solution)/shard_map/dot_general | solution.py:238
  145.3 0.0 copy-done.1
  145.3 0.0 copy-done.2
  145.4 1.3 fusion.4
  (3 shorter events, 0.0 us)
Async XLA Ops:
  0.0 2.8 %copy-start = (bf16[2880,8]{0,1:T(8,128)(2,1)S(1)}, bf16[2880,8]{0,1:T(8,128)(2,1)}, u32[]{:S(2)}) copy-start(bf16[2880,8]{0,1:T(8,128)(2,1)} %param.9) | copy-start | bytes 138244
  143.1 2.2 %copy-start.1 = (bf16[8,40,2880]{2,1,0:T(8,128)(2,1)S(1)}, bf16[8,40,2880]{2,1,0:T(8,128)(2,1)}, u32[]{:S(2)}) copy-start(bf16[8,40,2880]{2,1,0:T(8,128)(2,1)} %shard_map.65) | copy-start | bytes 5529604
  143.1 2.2 %copy-start.2 = (bf16[64,2880]{1,0:T(8,128)(2,1)S(1)}, bf16[64,2880]{1,0:T(8,128)(2,1)}, u32[]{:S(2)}) copy-start(bf16[64,2880]{1,0:T(8,128)(2,1)} %param.6) | copy-start | bytes 1105924
where the time goes:
time: 148 us; the launch traced here: 147 us
  Pallas kernels  124 us (84%)
  matrix products  17.8 us (12%)
  other arithmetic  4.4 us (3%)
    pallas_call x1, Pallas kernels, dispatch(): pl.pallas_call(functools.partial(dispatch_kernel, groups), out_shape=jax....  68.7 us
    pallas_call x1, Pallas kernels, collect(): pl.pallas_call(functools.partial(collect_kernel, groups), out_shape=jax.S...  55.6 us
    dot_general x1, matrix products, shards(): jnp.dot(rows_in, gate_up_weight[0], preferred_element_type=jnp.float32)  9.88 us
    dot_general x1, matrix products, shards(): lax.dot_general(placed.astype(jnp.bfloat16), normed, (((0,), (0,)), ((),...  3.03 us

commit v1 on v0

v1 whole, which is shorter than its diff:
```python
import functools

import jax
import jax.numpy as jnp
from jax import lax
from jax.experimental import pallas as pl
from jax.experimental.pallas import tpu as pltpu
from jax.sharding import PartitionSpec as P

SHARD = 4
LANES = 128
MESH = pl.DeviceIdType.MESH
ABSENT = -1024.0


def cuts(width, weights):
    tiles = width // LANES
    total = sum(weights)
    edges = [0]
    run = 0
    for w in weights:
        run += w
        edges.append(max(edges[-1] + 1, round(tiles * run / total)))
    edges[-1] = tiles
    return [(a * LANES, (b - a) * LANES) for a, b in zip(edges[:-1], edges[1:])]


def moe_kernel(
    planes, cols, capacity, fan_in, fan_out,
    tokens, routes, gain, router, gate_up_hbm, down_hbm,
    out,
    gate_up_raw, down_raw, gate_up, down, rank_all, tok_all, rows_in, other_in,
    hidden, act, part, mate_in, cross_in, pair, mix, mix_in,
    w_sem, rank_sem, z_sem, y_sem, x_sem, c_sem, c2_sem, x2_sem, y2_sem, z2_sem,
):
    f32 = jnp.float32
    bf16 = jnp.bfloat16
    me = lax.axis_index("ep")
    group = me // SHARD
    member = me % SHARD
    core = member % 2
    half = member // 2
    plane = group // cols
    col = group % cols
    experts = router.shape[1]
    toks, width = tokens.shape
    wide = tok_all.shape[1]
    ff = down_raw.shape[0]
    ffp = act.shape[1]
    sect = planes * capacity

    def device(p, c, h, k):
        return (p * cols + c) * SHARD + h * 2 + k

    mate = device(plane, col, half, 1 - core)
    across = device(plane, col, 1 - half, core)
    beside = device(plane, 1 - col, half, core)
    turns = sorted(range(1, planes), key=lambda r: min(r, planes - r))
    column = [device((plane + r) % planes, col, half, core) for r in turns]
    near = [mate, across, beside] + column

    loads = [
        pltpu.make_async_copy(gate_up_hbm, gate_up_raw, w_sem.at[0]),
        pltpu.make_async_copy(down_hbm, down_raw, w_sem.at[1]),
    ]
    for copy in loads:
        copy.start()

    barrier = pltpu.get_barrier_semaphore()
    for other in near:
        pl.semaphore_signal(barrier, inc=1, device_id={"ep": other}, device_id_type=MESH)

    def send(src, dst, sems, slot, target):
        return pltpu.make_async_remote_copy(
            src_ref=src, dst_ref=dst, send_sem=sems.at[0, slot], recv_sem=sems.at[1, slot],
            device_id={"ep": target}, device_id_type=MESH,
        )

    lane_e = lax.broadcasted_iota(jnp.int32, (toks, experts), 1)
    chosen = routes[...]
    hit = jnp.zeros((toks, experts), f32)
    for k in range(chosen.shape[1]):
        hit = hit + jnp.where(chosen[:, k : k + 1] == lane_e, 1.0, 0.0)
    lower = lax.broadcasted_iota(jnp.int32, (toks, toks), 1) < lax.broadcasted_iota(
        jnp.int32, (toks, toks), 0
    )
    rank = jnp.dot(
        jnp.where(lower, 1.0, 0.0).astype(bf16), hit.astype(bf16), preferred_element_type=f32
    )
    rank = jnp.where(hit > 0.0, rank, ABSENT)

    def lanes_from(value, base):
        select = lax.broadcasted_iota(jnp.int32, (experts, LANES), 1) == (
            lax.broadcasted_iota(jnp.int32, (experts, LANES), 0) + base
        )
        return jnp.dot(
            value.astype(bf16), jnp.where(select, 1.0, 0.0).astype(bf16),
            preferred_element_type=f32,
        )

    mine = pl.ds(pl.multiple_of(plane * toks, toks), toks)
    rank_all[mine, :] = lanes_from(rank, 0).astype(bf16)

    stream = tokens[...].astype(f32)
    mean_square = jnp.mean(stream * stream, axis=-1, keepdims=True)
    normed = (stream * lax.rsqrt(mean_square + 1e-05) * gain[...].astype(f32)).astype(bf16)
    tok_all[mine, wide - LANES : wide] = jnp.zeros((toks, LANES), bf16)
    tok_all[mine, 0:width] = normed

    pl.semaphore_wait(barrier, len(near))

    rank_copies = [
        send(rank_all.at[mine], rank_all.at[mine], rank_sem, i, column[i])
        for i in range(planes - 1)
    ]
    for copy in rank_copies:
        copy.start()
    z_copies = [
        [
            send(
                tok_all.at[mine, pl.ds(f0, fw)], tok_all.at[mine, pl.ds(f0, fw)],
                z_sem, k * (planes - 1) + i, column[i],
            )
            for i in range(planes - 1)
        ]
        for k, (f0, fw) in enumerate(fan_in)
    ]
    last = len(fan_in) - 1
    for k in range(last):
        for copy in z_copies[k]:
            copy.start()

    logits = jnp.dot(normed, router[...], preferred_element_type=f32)
    expo = jnp.where(hit > 0.0, jnp.exp(logits), 0.0)
    prob = expo / jnp.sum(expo, axis=-1, keepdims=True)
    high = prob.astype(bf16)
    low = (prob - high.astype(f32)).astype(bf16)
    base = LANES - (wide - width)
    tail = lanes_from(high, base) + lanes_from(low, base + experts)
    tok_all[mine, wide - LANES : wide] = (
        tok_all[mine, wide - LANES : wide].astype(f32) + tail
    ).astype(bf16)
    for copy in z_copies[last]:
        copy.start()

    expert = group
    expert_other = plane * cols + (1 - col)
    count = planes * toks
    for copy in rank_copies:
        copy.wait_recv()
    pick = lax.broadcasted_iota(jnp.int32, (16, LANES), 1) == jnp.where(
        lax.broadcasted_iota(jnp.int32, (16, LANES), 0) == 0, expert, expert_other
    )
    rank_rows = lax.dot_general(
        jnp.where(pick, 1.0, 0.0).astype(bf16), rank_all[...],
        (((1,), (1,)), ((), ())), preferred_element_type=f32,
    )
    block_of = (lax.broadcasted_iota(jnp.int32, (1, count), 1) // toks * capacity).astype(f32)
    slot_rows = lax.broadcasted_iota(jnp.int32, (sect, count), 0).astype(f32)
    gather = jnp.concatenate(
        [
            jnp.where(rank_rows[i : i + 1, :] + block_of == slot_rows, 1.0, 0.0).astype(bf16)
            for i in range(2)
        ],
        axis=0,
    )

    def section(j):
        return pl.ds(j * sect, sect)

    y_copies = [
        send(
            other_in.at[:, pl.ds(f0, fw)], rows_in.at[section(1), pl.ds(f0, fw)],
            y_sem, k, beside,
        )
        for k, (f0, fw) in enumerate(fan_in)
    ]
    x_copies = [
        [
            send(
                rows_in.at[section(j), pl.ds(f0, fw)], rows_in.at[section(2 + j), pl.ds(f0, fw)],
                x_sem, 2 * k + j, across,
            )
            for j in range(2)
        ]
        for k, (f0, fw) in enumerate(fan_in)
    ]
    c_copies = [
        [
            send(
                rows_in.at[section(j), pl.ds(f0, fw)], rows_in.at[section(4 + j), pl.ds(f0, fw)],
                c_sem, 4 * k + j, mate,
            )
            for j in range(4)
        ]
        for k, (f0, fw) in enumerate(fan_in)
    ]
    chunk = 2 * sect
    groups_in = 8 * sect // chunk

    def prepare():
        loads[0].wait()
        tile = 96
        steps = width // tile

        def move(i, carry):
            r = pl.ds(pl.multiple_of(i * tile, tile), tile)
            both = gate_up_raw[r, :].astype(f32)
            zero = jnp.zeros((tile, ffp - ff), f32)
            gate_up[r, 0:ffp] = jnp.concatenate([both[:, 0:ff], zero], axis=1).astype(bf16)
            gate_up[r, ffp : 2 * ffp] = jnp.concatenate([both[:, ff : 2 * ff], zero], axis=1).astype(
                bf16
            )
            return carry

        lax.fori_loop(0, steps, move, 0)
        gate_up[width:wide, :] = jnp.zeros((wide - width, 2 * ffp), bf16)
        loads[1].wait()
        down[:, wide - LANES : wide] = jnp.zeros((ffp, LANES), bf16)
        down[ff - ff % 16 : ffp, :] = jnp.zeros((ffp - ff + ff % 16, wide), bf16)
        down[0:ff, 0:width] = down_raw[...]

    def expand(k):
        f0, fw = fan_in[k]
        for j in range(4):
            c_copies[k][j].wait_recv()

        def one(g, carry):
            r = pl.ds(pl.multiple_of(g * chunk, chunk), chunk)
            value = jnp.dot(
                rows_in[r, f0 : f0 + fw], gate_up[f0 : f0 + fw, :], preferred_element_type=f32
            )
            if k == 0:
                hidden[r, :] = value
            else:
                hidden[r, :] += value
            return carry

        lax.fori_loop(0, groups_in, one, 0)

    def relay(k):
        for j in range(2):
            x_copies[k][j].wait_recv()
            c_copies[k][2 + j].start()

    for k, (f0, fw) in enumerate(fan_in):
        for copy in z_copies[k]:
            copy.wait_recv()
        value = jnp.dot(gather, tok_all[:, f0 : f0 + fw], preferred_element_type=f32).astype(bf16)
        other_in[:, f0 : f0 + fw] = value[sect : 2 * sect]
        rows_in[0:sect, f0 : f0 + fw] = value[0:sect]
        y_copies[k].start()
        x_copies[k][0].start()
        c_copies[k][0].start()
        if k == 0:
            prepare()
        y_copies[k].wait_recv()
        x_copies[k][1].start()
        c_copies[k][1].start()
        if k >= 1:
            relay(k - 1)
        if k >= 2:
            expand(k - 2)
    if last >= 1:
        expand(last - 1)
    relay(last)
    expand(last)

    lane_t = lax.broadcasted_iota(jnp.int32, (chunk, LANES), 1)
    is_prob = (lane_t == base + expert) | (lane_t == base + experts + expert)

    def activate(g, carry):
        r = pl.ds(pl.multiple_of(g * chunk, chunk), chunk)
        tails = rows_in[r, wide - LANES : wide].astype(f32)
        weight = jnp.sum(jnp.where(is_prob, tails, 0.0), axis=-1, keepdims=True)
        gate_part = hidden[r, 0:ffp]
        up_part = hidden[r, ffp : 2 * ffp]
        act[r, :] = (
            (up_part + 1.0) * gate_part * jax.nn.sigmoid(1.702 * gate_part) * weight
        ).astype(bf16)
        return carry

    lax.fori_loop(0, groups_in, activate, 0)

    lane_r = lax.broadcasted_iota(jnp.int32, (count, LANES), 1)
    ranks = rank_all[...].astype(f32)
    spot = [
        jnp.sum(jnp.where(lane_r == e, ranks, 0.0), axis=-1, keepdims=True)
        for e in (expert, expert_other)
    ]
    block_at = (lax.broadcasted_iota(jnp.int32, (count, 1), 0) // toks * capacity).astype(f32)
    lane_s = lax.broadcasted_iota(jnp.int32, (count, 2 * sect), 1)
    at = jnp.where(lane_s < sect, spot[0] + block_at, spot[1] + block_at + float(sect))
    keep = jnp.where(lane_s < sect, spot[0], spot[1]) >= 0.0
    scatter = jnp.where(keep & (at == lane_s.astype(f32)), 1.0, 0.0).astype(bf16)

    c2 = [
        [
            send(
                part.at[section(4 + j), pl.ds(f0, fw)], mate_in.at[section(j), pl.ds(f0, fw)],
                c2_sem, 4 * k + j, mate,
            )
            for j in range(4)
        ]
        for k, (f0, fw) in enumerate(fan_out)
    ]
    x2 = [
        [
            send(
                part.at[section(2 + j), pl.ds(f0, fw)], cross_in.at[section(j), pl.ds(f0, fw)],
                x2_sem, 2 * k + j, across,
            )
            for j in range(2)
        ]
        for k, (f0, fw) in enumerate(fan_out)
    ]
    y2 = [
        send(
            part.at[section(1), pl.ds(f0, fw)], pair.at[section(1), pl.ds(f0, fw)],
            y2_sem, k, beside,
        )
        for k, (f0, fw) in enumerate(fan_out)
    ]
    z2 = [
        [
            send(
                mix.at[
                    pl.ds(pl.multiple_of((plane + turns[i]) % planes * toks, toks), toks),
                    pl.ds(f0, fw),
                ],
                mix_in.at[i, :, pl.ds(f0, fw)],
                z2_sem, k * (planes - 1) + i, column[i],
            )
            for i in range(planes - 1)
        ]
        for k, (f0, fw) in enumerate(fan_out)
    ]

    def contract(k):
        f0, fw = fan_out[k]

        def one(i, carry):
            g = groups_in - 1 - i
            r = pl.ds(pl.multiple_of(g * chunk, chunk), chunk)
            part[r, f0 : f0 + fw] = jnp.dot(
                act[r, :], down[:, f0 : f0 + fw], preferred_element_type=f32
            ).astype(bf16)
            return carry

        lax.fori_loop(0, groups_in, one, 0)
        for j in (2, 3, 0, 1):
            c2[k][j].start()

    def add_mate(k):
        f0, fw = fan_out[k]
        for j in (2, 3, 0, 1):
            c2[k][j].wait_recv()
            a = part[j * sect : (j + 1) * sect, f0 : f0 + fw].astype(f32)
            b = mate_in[j * sect : (j + 1) * sect, f0 : f0 + fw].astype(f32)
            part[j * sect : (j + 1) * sect, f0 : f0 + fw] = (a + b).astype(bf16)
            if j >= 2:
                x2[k][j - 2].start()

    def add_across(k):
        f0, fw = fan_out[k]
        x2[k][1].wait_recv()
        a = part[sect : 2 * sect, f0 : f0 + fw].astype(f32)
        b = cross_in[sect : 2 * sect, f0 : f0 + fw].astype(f32)
        part[sect : 2 * sect, f0 : f0 + fw] = (a + b).astype(bf16)
        y2[k].start()
        x2[k][0].wait_recv()
        a = part[0:sect, f0 : f0 + fw].astype(f32)
        b = cross_in[0:sect, f0 : f0 + fw].astype(f32)
        pair[0:sect, f0 : f0 + fw] = (a + b).astype(bf16)

    def to_tokens(k):
        f0, fw = fan_out[k]
        y2[k].wait_recv()
        mix[:, f0 : f0 + fw] = jnp.dot(
            scatter, pair[:, f0 : f0 + fw], preferred_element_type=f32
        ).astype(bf16)
        for copy in z2[k]:
            copy.start()

    def finish(k):
        f0, fw = fan_out[k]
        f1 = min(f0 + fw, width)
        for copy in z2[k]:
            copy.wait_recv()
        total = mix[mine, f0:f1].astype(f32)
        for i in range(planes - 1):
            total = total + mix_in[i, :, f0:f1].astype(f32)
        out[:, f0:f1] = (tokens[:, f0:f1].astype(f32) + total).astype(bf16)

    ends = len(fan_out)
    for k in range(ends + 3):
        if k < ends:
            contract(k)
        if 1 <= k <= ends:
            add_mate(k - 1)
        if 2 <= k <= ends + 1:
            add_across(k - 2)
        if 3 <= k <= ends + 2:
            to_tokens(k - 3)
    for k in range(ends):
        finish(k)

    for copy in rank_copies + y_copies + y2:
        copy.wait_send()
    for many in z_copies + x_copies + c_copies + c2 + x2 + z2:
        for copy in many:
            copy.wait_send()


def shards(tokens, routes, norm_gain, router_weight, gate_up_weight, down_weight):
    toks, width = tokens.shape
    top_count = routes.shape[1]
    experts = router_weight.shape[1]
    devices = lax.axis_size("ep")
    groups = devices // SHARD
    cols = 2
    planes = groups // cols
    ff = down_weight.shape[1]
    capacity = min(toks, SHARD * (17 * toks * top_count // (16 * experts * SHARD) + 1))
    wide = -(-(width + 2 * experts) // LANES) * LANES
    ffp = -(-ff // LANES) * LANES
    sect = planes * capacity
    fan_in = cuts(wide, [2, 4, 6, 6, 3, 2])
    fan_out = cuts(wide, [3, 6, 6, 5, 3])
    n_in, n_out = len(fan_in), len(fan_out)
    bf16 = jnp.bfloat16
    vmem = pl.BlockSpec(memory_space=pltpu.VMEM)
    hbm = pl.BlockSpec(memory_space=pl.ANY)
    dma = lambda n: pltpu.SemaphoreType.DMA((2, n))
    return pl.pallas_call(
        functools.partial(moe_kernel, planes, cols, capacity, fan_in, fan_out),
        out_shape=jax.ShapeDtypeStruct((toks, width), bf16),
        in_specs=[vmem, vmem, vmem, vmem, hbm, hbm],
        out_specs=vmem,
        scratch_shapes=[
            pltpu.VMEM((width, 2 * ff), bf16),
            pltpu.VMEM((ff, width), bf16),
            pltpu.VMEM((wide, 2 * ffp), bf16),
            pltpu.VMEM((ffp, wide), bf16),
            pltpu.VMEM((planes * toks, LANES), bf16),
            pltpu.VMEM((planes * toks, wide), bf16),
            pltpu.VMEM((8 * sect, wide), bf16),
            pltpu.VMEM((sect, wide), bf16),
            pltpu.VMEM((8 * sect, 2 * ffp), jnp.float32),
            pltpu.VMEM((8 * sect, ffp), bf16),
            pltpu.VMEM((8 * sect, wide), bf16),
            pltpu.VMEM((4 * sect, wide), bf16),
            pltpu.VMEM((2 * sect, wide), bf16),
            pltpu.VMEM((2 * sect, wide), bf16),
            pltpu.VMEM((planes * toks, wide), bf16),
            pltpu.VMEM((planes - 1, toks, wide), bf16),
            pltpu.SemaphoreType.DMA((2,)),
            dma(planes - 1),
            dma(n_in * (planes - 1)),
            dma(n_in),
            dma(2 * n_in),
            dma(4 * n_in),
            dma(4 * n_out),
            dma(2 * n_out),
            dma(n_out),
            dma(n_out * (planes - 1)),
        ],
        compiler_params=pltpu.CompilerParams(
            collective_id=0, has_side_effects=True, vmem_limit_bytes=63 * 1024 * 1024
        ),
    )(
        tokens,
        routes,
        norm_gain.reshape(1, width),
        router_weight,
        gate_up_weight[0],
        down_weight[0],
    )


def solution(mesh):
    in_specs = (
        P(("groups", "ep"), None),
        P(("groups", "ep"), None),
        P(),
        P(),
        P("ep", None, None),
        P("ep", None, None),
    )
    out_specs = P(("groups", "ep"), None)
    return jax.shard_map(shards, mesh=mesh, in_specs=in_specs, out_specs=out_specs, check_vma=False)
```

time: 148 us -> 141 us (0.953)
  matrix products: 17.8 us -> 0 us
  local copies, waits for them, and re-layouts: 0.1 us -> 12.9 us
  other arithmetic: 4.4 us -> 0 us
  Pallas kernels: 124 us -> 128 us
    dot_general x6 -> x0, matrix products: 17.8 us -> none  [the longest x1 9.88 us: shards(): jnp.dot(rows_in, gate_up_weight[0], preferred_element_type=jnp.float32)]
    unnamed x6 -> x4, local copies, waits for them, and re-layouts: 0.01 us -> 11.6 us
    pallas_call x2 -> x1, Pallas kernels: 124 us -> 128 us  [shards(): pl.pallas_call(functools.partial(moe_kernel, planes, cols, capacity, fan_...]
    convert_element_type x2 -> x0, other arithmetic: 2.39 us -> none  [the longest x1 1.69 us: shards(): ((up_part + 1.0) * gate_part * jax.nn.sigmoid(1.702 * gate_part)).astype(...]
where the time goes in v1:
time: 141 us
  Pallas kernels  128 us (91%)
  local copies, waits for them, and re-layouts  12.9 us (9%)
    pallas_call x1, Pallas kernels, shards(): pl.pallas_call(functools.partial(moe_kernel, planes, cols, capacity, fan_...  128 us
    unnamed x4, local copies, waits for them, and re-layouts  11.6 us

profile of v1, /device:TPU:0, one launch (start us, length us, event | category | flops | bytes accessed | tf_op | source)
XLA Modules:
  0.0 141.0 jit_solution(13183778825867091617)
XLA Ops:
  0.0 1.3 reshape.3.gain
  1.3 1.4 copy.8.routes
  2.7 1.9 %copy.9.router = bf16[2880,8]{1,0:T(8,128)(2,1)} copy(bf16[2880,8]{0,1:T(8,128)(2,1)} %param.9) | data formatting | bytes 92160 | tf_op args[3]
  4.6 6.5 %copy.7 = bf16[1,2880,720]{2,1,0:T(8,128)(2,1)} copy(bf16[1,2880,720]{1,2,0:T(8,128)(2,1)} %param.10) | data formatting | bytes 8294400 | tf_op args[4]
  11.1 128.1 %shard_map.64 = bf16[64,2880]{1,0:T(8,128)(2,1)} custom-call(bf16[64,2880]{1,0:T(8,128)(2,1)} %tokens.1, s32[64,4]{1,0:T(8,128)} %copy.8.routes, bf16[1,2880]{1,0:T(2,128)(2,1)} %reshape.3.gain, bf16[2880,8]{1,0:T(8,128)(2,1)} %copy.9.router, bf16[2880,720]{1,0:T(8,128)(2,1)} %bitcast.2, bf16[360,2880]{1,0:T(8,128)(2,1)} %bitcast.3), custom_call_target="tpu_custom_call" | custom-call | tf_op jit(solution)/shard_map/pallas_call | solution.py:435
  139.2 1.8 %copy.11 = bf16[64,2880]{1,0:T(8,128)(2,1)} copy(bf16[64,2880]{1,0:T(8,128)(2,1)} %shard_map.64) | data formatting | bytes 737280

commit v2 on v1

v2 whole, which is shorter than its diff:
```python
import functools

import jax
import jax.numpy as jnp
from jax import lax
from jax.experimental import pallas as pl
from jax.experimental.pallas import tpu as pltpu
from jax.sharding import PartitionSpec as P

SHARD = 4
LANES = 128
MESH = pl.DeviceIdType.MESH
ABSENT = -1024.0
FAN_IN = ((2, "direct"), (3, "narrow"), (3, "narrow"), (4, "narrow"), (5, "narrow"), (3, "wide"), (3, "wide"))
FAN_OUT = ((1, "narrow"), (2, "wide"), (4, "wide"), (6, "narrow"), (5, "narrow"), (5, "direct"))
ORDER = (
    "S1", "S2", "S0", "W5", "R2", "L", "S3", "W6",
    "R1", "G2", "S4", "G0", "G1", "R3", "Y2", "Y1",
    "G3", "S6", "R4", "SX6", "X1", "X2", "G4", "SX5",
    "R6", "RX6", "G6", "S5", "Y4", "C1", "RX5", "GX6",
    "SC", "C2", "Y0", "GX5", "Y3", "R5", "X4", "G5",
    "X0", "YX6", "Y6", "C4", "YX5", "C6", "X3", "C0",
    "Y5", "C3", "C5", "A", "e0", "e1", "e3", "m0",
    "m1", "e2", "m3", "m2", "x0", "t1", "tx1", "t2",
    "e4", "e5", "x3", "m4", "t0", "r1", "m5", "rx1",
    "r2", "r0", "tx2", "t3", "rx2", "x4", "f0", "r3",
    "x5", "t4", "r4", "xl2", "f3", "f2", "t5", "xl1",
    "f1", "f4", "f5",
)


def cuts(width, plan):
    tiles = width // LANES
    total = sum(weight for weight, _ in plan)
    pieces = [max(1, tiles * weight // total) for weight, _ in plan]
    while sum(pieces) != tiles:
        step = 1 if sum(pieces) < tiles else -1
        gap = [step * (weight * tiles / total - piece) for piece, (weight, _) in zip(pieces, plan)]
        pieces[gap.index(max(gap))] += step
    wide_at = sum(p for p, (_, kind) in zip(pieces, plan) if kind != "wide") * LANES
    narrow_at = 0
    spans = []
    for piece, (_, kind) in zip(pieces, plan):
        size = piece * LANES
        if kind == "wide":
            spans.append((wide_at, size, kind))
            wide_at += size
        else:
            spans.append((narrow_at, size, kind))
            narrow_at += size
    return spans


def wide_span(spans):
    wide = [(f0, fw) for f0, fw, kind in spans if kind == "wide"]
    return min(f0 for f0, _ in wide), sum(fw for _, fw in wide)


def moe_kernel(
    planes, cols, capacity, fan_in, fan_out,
    tokens, routes, gain, router, gate_up_hbm, down_hbm,
    out,
    gate_up, down_raw, down, rank_all, rank_x, tok_all, tok_x, rows_in, other_in,
    hidden, act, part, mate_in, cross_in, pair, pair_x, mix, mix_x, mix_in, mix_x_in, total,
    final_x, final_x_in,
    w_sem, rank_sem, w_x_sem, z_sem, y_sem, x_sem, c_sem, c2_sem, x2_sem, y2_sem, z2_sem, w_x2_sem,
):
    f32 = jnp.float32
    bf16 = jnp.bfloat16
    me = lax.axis_index("ep")
    group = me // SHARD
    member = me % SHARD
    core = member % 2
    half = member // 2
    plane = group // cols
    col = group % cols
    experts = router.shape[0]
    toks, width = tokens.shape
    wide = tok_all.shape[1]
    ff = down_raw.shape[0]
    ffp = act.shape[1]
    sect = planes * capacity
    count = planes * toks
    reach = planes - 1
    dirs = (1, -1)
    in_x = wide_span(fan_in)[0]
    out_x = wide_span(fan_out)[0]

    def device(p, c, h, k):
        return (p * cols + c) * SHARD + h * 2 + k

    mate = device(plane, col, half, 1 - core)
    across = device(plane, col, 1 - half, core)
    beside = device(plane, 1 - col, half, core)
    turns = sorted(range(1, planes), key=lambda r: min(r, planes - r))
    column = [device((plane + r) % planes, col, half, core) for r in turns]
    column_x = [device((plane + r) % planes, col, 1 - half, core) for r in turns]
    near = [mate, across, beside] + column + column_x

    def inside(p):
        return (p >= 0) & (p < planes)

    def clip(p):
        return jnp.clip(p, 0, planes - 1)

    for i in range(2):
        gate_up[(i + 1) * ffp - LANES : (i + 1) * ffp, :] = jnp.zeros((LANES, width), bf16)
    loads = [
        pltpu.make_async_copy(
            gate_up_hbm.at[pl.ds(i * ff, ff)], gate_up.at[pl.ds(i * ffp, ff)], w_sem.at[i]
        )
        for i in range(2)
    ] + [pltpu.make_async_copy(down_hbm, down_raw, w_sem.at[2])]
    for copy in loads:
        copy.start()

    barrier = pltpu.get_barrier_semaphore()
    for other in near:
        pl.semaphore_signal(barrier, inc=1, device_id={"ep": other}, device_id_type=MESH)

    def send(src, dst, sems, slot, target):
        return pltpu.make_async_remote_copy(
            src_ref=src, dst_ref=dst, send_sem=sems.at[0, slot], recv_sem=sems.at[1, slot],
            device_id={"ep": target}, device_id_type=MESH,
        )

    def block(p):
        return pl.ds(pl.multiple_of(p * toks, toks), toks)

    row_e = lax.broadcasted_iota(jnp.int32, (experts, toks), 0)
    chosen = routes[...]
    hit_rows = jnp.zeros((experts, toks), f32)
    for k in range(chosen.shape[0]):
        hit_rows = hit_rows + jnp.where(chosen[k : k + 1, :] == row_e, 1.0, 0.0)
    at_col = lax.broadcasted_iota(jnp.int32, (toks, toks), 1)
    at_row = lax.broadcasted_iota(jnp.int32, (toks, toks), 0)

    def by_token(mask):
        return lax.dot_general(
            jnp.where(mask, 1.0, 0.0).astype(bf16), hit_rows.astype(bf16),
            (((1,), (1,)), ((), ())), preferred_element_type=f32,
        )

    hit = by_token(at_col == at_row)
    rank = jnp.where(hit > 0.0, by_token(at_col < at_row), ABSENT)

    def lanes_from(value, base):
        select = lax.broadcasted_iota(jnp.int32, (experts, LANES), 1) == (
            lax.broadcasted_iota(jnp.int32, (experts, LANES), 0) + base
        )
        return jnp.dot(
            value.astype(bf16), jnp.where(select, 1.0, 0.0).astype(bf16),
            preferred_element_type=f32,
        )

    mine = block(plane)
    rank_all[mine, :] = lanes_from(rank, 0).astype(bf16)

    stream = tokens[...].astype(f32)
    mean_square = jnp.mean(stream * stream, axis=-1, keepdims=True)
    normed = (stream * lax.rsqrt(mean_square + 1e-05) * gain[...].astype(f32)[None, :]).astype(bf16)
    tok_all[mine, wide - LANES : wide] = jnp.zeros((toks, LANES), bf16)
    tok_all[mine, 0:width] = normed

    pl.semaphore_wait(barrier, len(near))

    rank_copies = [
        send(rank_all.at[mine], rank_all.at[mine], rank_sem, i, column[i]) for i in range(reach)
    ]
    rank_x_copies = [
        send(rank_all.at[mine], rank_x.at[mine], rank_sem, reach + i, target)
        for i, target in enumerate([across] + column_x)
    ]

    lanes_of = {}
    for k, (f0, fw, kind) in enumerate(fan_in):
        lanes_of[k] = [(tok_all, f0, fw, 2 * k)]
        if kind == "wide":
            lanes_of[k].append((tok_x, f0 - in_x, fw, 2 * k + 1))

    def z_copy(k, lane, s, d):
        ref, a, fw, at = lanes_of[k][lane]
        relayed = d >= 3 and fan_in[k][2] != "direct"
        source = block(clip(plane - s * (d - 1))) if relayed else mine
        target = clip(plane + (s if relayed else s * d))
        view = ref.at[source, pl.ds(a, fw)]
        slot = (at * 2 + (s + 1) // 2) * reach + d - 1
        return send(view, view, z_sem, slot, device(target, col, half, core))

    def z_sends(k, d, s):
        if d >= 3 and fan_in[k][2] != "direct":
            return inside(plane - s * (d - 1)) & inside(plane + s)
        return inside(plane + s * d)

    def z_start(k, lane):
        direct = fan_in[k][2] == "direct"
        for d in range(reach if direct else min(2, reach), 0, -1):
            for s in dirs:
                pl.when(z_sends(k, d, s))(z_copy(k, lane, s, d).start)

    def z_relay(k, lane):
        if fan_in[k][2] == "direct":
            return
        for d in range(3, planes):
            for s in dirs:

                @pl.when(z_sends(k, d, s))
                def _():
                    z_copy(k, lane, s, d - 1).wait_recv()
                    z_copy(k, lane, s, d).start()

    def z_arrive(k, lane):
        for d in range(1, planes):
            for s in dirs:
                come = inside(plane - s * d)
                if d >= 2 and d < reach and fan_in[k][2] != "direct":
                    come = come & ~inside(plane + s)
                pl.when(come)(z_copy(k, lane, s, d).wait_recv)

    def z_drain(k, lane):
        for d in range(1, planes):
            for s in dirs:
                pl.when(z_sends(k, d, s))(z_copy(k, lane, s, d).wait_send)

    for copy in rank_copies + rank_x_copies:
        copy.start()
    w_x_copies = {}
    for k, (f0, fw, kind) in enumerate(fan_in):
        if kind == "wide":
            w_x_copies[k] = send(
                tok_all.at[mine, pl.ds(f0, fw)], tok_x.at[mine, pl.ds(f0 - in_x, fw)],
                w_x_sem, k, across,
            )
    base = LANES - (wide - width)

    def add_prob():
        logits = lax.dot_general(
            normed, router[...], (((1,), (1,)), ((), ())), preferred_element_type=f32
        )
        expo = jnp.where(hit > 0.0, jnp.exp(logits), 0.0)
        prob = expo / jnp.sum(expo, axis=-1, keepdims=True)
        high = prob.astype(bf16)
        low = (prob - high.astype(f32)).astype(bf16)
        tail = lanes_from(high, base) + lanes_from(low, base + experts)
        tok_all[mine, wide - LANES : wide] = (
            tok_all[mine, wide - LANES : wide].astype(f32) + tail
        ).astype(bf16)

    expert = group
    expert_other = plane * cols + (1 - col)

    def gather_of(ranks):
        pick = lax.broadcasted_iota(jnp.int32, (16, LANES), 1) == jnp.where(
            lax.broadcasted_iota(jnp.int32, (16, LANES), 0) == 0, expert, expert_other
        )
        rank_rows = lax.dot_general(
            jnp.where(pick, 1.0, 0.0).astype(bf16), ranks[...],
            (((1,), (1,)), ((), ())), preferred_element_type=f32,
        )
        block_of = (lax.broadcasted_iota(jnp.int32, (1, count), 1) // toks * capacity).astype(f32)
        slot_rows = lax.broadcasted_iota(jnp.int32, (sect, count), 0).astype(f32)
        return jnp.concatenate(
            [
                jnp.where(rank_rows[i : i + 1, :] + block_of == slot_rows, 1.0, 0.0).astype(bf16)
                for i in range(2)
            ],
            axis=0,
        )

    def scatter_of(ranks_ref):
        lane_r = lax.broadcasted_iota(jnp.int32, (count, LANES), 1)
        ranks = ranks_ref[...].astype(f32)
        spot = [
            jnp.sum(jnp.where(lane_r == e, ranks, 0.0), axis=-1, keepdims=True)
            for e in (expert, expert_other)
        ]
        block_at = (lax.broadcasted_iota(jnp.int32, (count, 1), 0) // toks * capacity).astype(f32)
        lane_s = lax.broadcasted_iota(jnp.int32, (count, 2 * sect), 1)
        at = jnp.where(lane_s < sect, spot[0] + block_at, spot[1] + block_at + float(sect))
        keep = jnp.where(lane_s < sect, spot[0], spot[1]) >= 0.0
        return jnp.where(keep & (at == lane_s.astype(f32)), 1.0, 0.0).astype(bf16)

    def section(j):
        return pl.ds(j * sect, sect)

    y_copies = [
        [
            send(
                other_in.at[section(i), pl.ds(f0, fw)],
                rows_in.at[section(1 + 2 * i), pl.ds(f0, fw)],
                y_sem, 2 * k + i, beside,
            )
            for i in range(2 if kind == "wide" else 1)
        ]
        for k, (f0, fw, kind) in enumerate(fan_in)
    ]
    x_copies = [
        [
            send(
                rows_in.at[section(j), pl.ds(f0, fw)], rows_in.at[section(2 + j), pl.ds(f0, fw)],
                x_sem, 2 * k + j, across,
            )
            for j in range(0 if kind == "wide" else 2)
        ]
        for k, (f0, fw, kind) in enumerate(fan_in)
    ]
    c_copies = [
        [
            send(
                rows_in.at[section(j), pl.ds(f0, fw)], rows_in.at[section(4 + j), pl.ds(f0, fw)],
                c_sem, 4 * k + j, mate,
            )
            for j in range(4)
        ]
        for k, (f0, fw, _) in enumerate(fan_in)
    ]
    chunk = 2 * sect
    groups_in = 8 * sect // chunk

    def prepare():
        for copy in loads:
            copy.wait()
        down[:, wide - LANES : wide] = jnp.zeros((ffp, LANES), bf16)
        down[ff - ff % 16 : ffp, :] = jnp.zeros((ffp - ff + ff % 16, wide), bf16)
        down[0:ff, 0:width] = down_raw[...]

    def cross_first(k):
        w_x_copies[k].wait_recv()
        z_start(k, 1)

    gathers = {}

    def gather_rows(k):
        f0, fw, kind = fan_in[k]
        if 0 not in gathers:
            for copy in rank_copies:
                copy.wait_recv()
            gathers[0] = gather_of(rank_all)
        z_arrive(k, 0)
        value = jnp.dot(
            gathers[0], tok_all[:, f0 : f0 + fw], preferred_element_type=f32
        ).astype(bf16)
        other_in[0:sect, f0 : f0 + fw] = value[sect : 2 * sect]
        rows_in[0:sect, f0 : f0 + fw] = value[0:sect]
        y_copies[k][0].start()
        if kind != "wide":
            x_copies[k][0].start()
        c_copies[k][0].start()

    def gather_rows_x(k):
        f0, fw, kind = fan_in[k]
        if 1 not in gathers:
            for copy in rank_x_copies:
                copy.wait_recv()
            gathers[1] = gather_of(rank_x)
        z_arrive(k, 1)
        a = f0 - in_x
        value = jnp.dot(gathers[1], tok_x[:, a : a + fw], preferred_element_type=f32).astype(bf16)
        other_in[sect : 2 * sect, f0 : f0 + fw] = value[sect : 2 * sect]
        rows_in[2 * sect : 3 * sect, f0 : f0 + fw] = value[0:sect]
        y_copies[k][1].start()
        c_copies[k][2].start()

    def from_beside(k, i):
        y_copies[k][i].wait_recv()
        if fan_in[k][2] != "wide":
            x_copies[k][1].start()
        c_copies[k][1 + 2 * i].start()

    def from_across(k):
        for j, copy in enumerate(x_copies[k]):
            copy.wait_recv()
            c_copies[k][2 + j].start()

    done_in = []

    def expand(k):
        f0, fw, _ = fan_in[k]
        f1 = min(f0 + fw, width)
        for j in range(4):
            c_copies[k][j].wait_recv()
        first = not done_in
        if first:
            prepare()
        done_in.append(k)

        def one(g, carry):
            r = pl.ds(pl.multiple_of(g * chunk, chunk), chunk)
            value = lax.dot_general(
                rows_in[r, f0:f1], gate_up[:, f0:f1], (((1,), (1,)), ((), ())),
                preferred_element_type=f32,
            )
            if first:
                hidden[r, :] = value
            else:
                hidden[r, :] += value
            return carry

        lax.fori_loop(0, groups_in, one, 0)

    n_in = len(fan_in)
    lane_t = lax.broadcasted_iota(jnp.int32, (chunk, LANES), 1)
    is_prob = (lane_t == base + expert) | (lane_t == base + experts + expert)

    def activate_group(g, carry):
        r = pl.ds(pl.multiple_of(g * chunk, chunk), chunk)
        tails = rows_in[r, wide - LANES : wide].astype(f32)
        weight = jnp.sum(jnp.where(is_prob, tails, 0.0), axis=-1, keepdims=True)
        gate_part = hidden[r, 0:ffp]
        up_part = hidden[r, ffp : 2 * ffp]
        act[r, :] = (
            (up_part + 1.0) * gate_part * jax.nn.sigmoid(1.702 * gate_part) * weight
        ).astype(bf16)
        return carry

    def activate():
        lax.fori_loop(0, groups_in, activate_group, 0)

    n_out = len(fan_out)
    c2 = [
        [
            send(
                part.at[section(4 + j), pl.ds(f0, fw)], mate_in.at[section(j), pl.ds(f0, fw)],
                c2_sem, 4 * k + j, mate,
            )
            for j in range(4)
        ]
        for k, (f0, fw, _) in enumerate(fan_out)
    ]
    x2 = [
        [
            send(
                part.at[section(2 + j), pl.ds(f0, fw)], cross_in.at[section(j), pl.ds(f0, fw)],
                x2_sem, 2 * k + j, across,
            )
            for j in range(0 if kind == "wide" else 2)
        ]
        for k, (f0, fw, kind) in enumerate(fan_out)
    ]
    y2 = [
        [send(part.at[section(1), pl.ds(f0, fw)], pair.at[section(1), pl.ds(f0, fw)], y2_sem, 2 * k, beside)]
        for k, (f0, fw, _) in enumerate(fan_out)
    ]
    lanes_to = {}
    for k, (f0, fw, kind) in enumerate(fan_out):
        lanes_to[k] = [(mix, mix_in, f0, fw, 2 * k)]
        if kind == "wide":
            a = f0 - out_x
            y2[k].append(
                send(
                    part.at[section(3), pl.ds(f0, fw)], pair_x.at[section(1), pl.ds(a, fw)],
                    y2_sem, 2 * k + 1, beside,
                )
            )
            lanes_to[k].append((mix_x, mix_x_in, a, fw, 2 * k + 1))
    w_x2 = {
        k: send(
            final_x.at[:, pl.ds(f0 - out_x, fw)], final_x_in.at[:, pl.ds(f0 - out_x, fw)],
            w_x2_sem, k, across,
        )
        for k, (f0, fw, kind) in enumerate(fan_out)
        if kind == "wide"
    }

    def z2_copy(k, lane, s, d):
        src, dst, a, fw, at = lanes_to[k][lane]
        relayed = d >= 3 and fan_out[k][2] != "direct"
        target = clip(plane - (s if relayed else s * d))
        spot = (s + 1) // 2 * reach + d - 1
        return send(
            src.at[block(clip(plane - s * d)), pl.ds(a, fw)], dst.at[spot, :, pl.ds(a, fw)],
            z2_sem, at * 2 * reach + spot, device(target, col, half, core),
        )

    def z2_adds(k, s, d):
        if d < 2 or d >= reach or fan_out[k][2] == "direct":
            return None
        return inside(plane + s)

    def z2_start(k, lane):
        for d in range(reach, 0, -1):
            for s in dirs:
                go = inside(plane - s * d)
                adds = z2_adds(k, s, d)
                if adds is not None:
                    go = go & ~adds
                pl.when(go)(z2_copy(k, lane, s, d).start)

    def z2_relay(k, lane):
        src, dst, a, fw, _ = lanes_to[k][lane]
        for d in range(reach - 1, 1, -1):
            for s in dirs:
                adds = z2_adds(k, s, d)
                if adds is None:
                    continue

                @pl.when(inside(plane - s * d) & adds)
                def _():
                    z2_copy(k, lane, s, d + 1).wait_recv()
                    rows = block(clip(plane - s * d))
                    spot = (s + 1) // 2 * reach + d
                    src[rows, a : a + fw] = (
                        src[rows, a : a + fw].astype(f32) + dst[spot, :, a : a + fw].astype(f32)
                    ).astype(bf16)
                    z2_copy(k, lane, s, d).start()

    def z2_sum(k, lane):
        src, dst, a, fw, _ = lanes_to[k][lane]
        total[:, 0:fw] = src[mine, a : a + fw].astype(f32)
        far = reach if fan_out[k][2] == "direct" else min(2, reach)
        for d in range(1, far + 1):
            for s in dirs:

                @pl.when(inside(plane + s * d))
                def _():
                    z2_copy(k, lane, s, d).wait_recv()
                    spot = (s + 1) // 2 * reach + d - 1
                    total[:, 0:fw] += dst[spot, :, a : a + fw].astype(f32)

    def z2_drain(k, lane):
        for d in range(1, planes):
            for s in dirs:
                pl.when(inside(plane - s * d))(z2_copy(k, lane, s, d).wait_send)

    def contract(k):
        f0, fw, _ = fan_out[k]

        def one(i, carry):
            g = groups_in - 1 - i
            r = pl.ds(pl.multiple_of(g * chunk, chunk), chunk)
            part[r, f0 : f0 + fw] = jnp.dot(
                act[r, :], down[:, f0 : f0 + fw], preferred_element_type=f32
            ).astype(bf16)
            return carry

        lax.fori_loop(0, groups_in, one, 0)
        for j in (3, 2, 1, 0):
            c2[k][j].start()

    def plus(a, b):
        return (a.astype(f32) + b.astype(f32)).astype(bf16)

    def add_mate(k):
        f0, fw, kind = fan_out[k]
        for j in (3, 1, 2, 0) if kind == "wide" else (3, 2, 1, 0):
            c2[k][j].wait_recv()
            r = slice(j * sect, (j + 1) * sect)
            value = plus(part[r, f0 : f0 + fw], mate_in[r, f0 : f0 + fw])
            if kind != "wide":
                part[r, f0 : f0 + fw] = value
                if j >= 2:
                    x2[k][j - 2].start()
            elif j % 2 == 1:
                part[r, f0 : f0 + fw] = value
                y2[k][j // 2].start()
            elif j == 0:
                pair[0:sect, f0 : f0 + fw] = value
            else:
                pair_x[0:sect, f0 - out_x : f0 - out_x + fw] = value

    def add_across(k):
        f0, fw, kind = fan_out[k]
        x2[k][1].wait_recv()
        r = slice(sect, 2 * sect)
        part[r, f0 : f0 + fw] = plus(part[r, f0 : f0 + fw], cross_in[r, f0 : f0 + fw])
        y2[k][0].start()

    scatters = {}

    def place():
        scatters[0] = scatter_of(rank_all)
        scatters[1] = scatter_of(rank_x)

    def to_tokens(k):
        f0, fw, kind = fan_out[k]
        if kind != "wide":
            x2[k][0].wait_recv()
            r = slice(0, sect)
            pair[r, f0 : f0 + fw] = plus(part[r, f0 : f0 + fw], cross_in[r, f0 : f0 + fw])
        y2[k][0].wait_recv()
        mix[:, f0 : f0 + fw] = jnp.dot(
            scatters[0], pair[:, f0 : f0 + fw], preferred_element_type=f32
        ).astype(bf16)
        z2_start(k, 0)

    def to_tokens_x(k):
        f0, fw, kind = fan_out[k]
        y2[k][1].wait_recv()
        a = f0 - out_x
        mix_x[:, a : a + fw] = jnp.dot(
            scatters[1], pair_x[:, a : a + fw], preferred_element_type=f32
        ).astype(bf16)
        z2_start(k, 1)

    def cross_last(k):
        f0, fw, kind = fan_out[k]
        a = f0 - out_x
        z2_sum(k, 1)
        final_x[:, a : a + fw] = total[:, 0:fw].astype(bf16)
        w_x2[k].start()

    def finish(k):
        f0, fw, kind = fan_out[k]
        f1 = min(f0 + fw, width)
        z2_sum(k, 0)
        value = tokens[:, f0:f1].astype(f32) + total[:, 0 : f1 - f0]
        if kind == "wide":
            w_x2[k].wait_recv()
            value = value + final_x_in[:, f0 - out_x : f1 - out_x].astype(f32)
        out[:, f0:f1] = value.astype(bf16)

    steps = {
        "L": add_prob,
        "A": activate,
        "SC": place,
        "W": lambda k: w_x_copies[k].start(),
        "S": lambda k: z_start(k, 0),
        "R": lambda k: z_relay(k, 0),
        "G": gather_rows,
        "SX": cross_first,
        "RX": lambda k: z_relay(k, 1),
        "GX": gather_rows_x,
        "Y": lambda k: from_beside(k, 0),
        "YX": lambda k: from_beside(k, 1),
        "X": from_across,
        "C": expand,
        "e": contract,
        "m": add_mate,
        "x": add_across,
        "t": to_tokens,
        "tx": to_tokens_x,
        "r": lambda k: z2_relay(k, 0),
        "rx": lambda k: z2_relay(k, 1),
        "xl": cross_last,
        "f": finish,
    }
    for word in ORDER:
        name = word.rstrip("0123456789")
        steps[name](*([int(word[len(name) :])] if word != name else []))

    for copy in rank_copies + rank_x_copies + list(w_x_copies.values()) + list(w_x2.values()):
        copy.wait_send()
    for many in y_copies + x_copies + c_copies + c2 + x2 + y2:
        for copy in many:
            copy.wait_send()
    for k in range(n_in):
        for lane in range(len(lanes_of[k])):
            z_drain(k, lane)
    for k in range(n_out):
        for lane in range(len(lanes_to[k])):
            z2_drain(k, lane)


def shards(tokens, routes, norm_gain, router_weight, gate_up_weight, down_weight):
    toks, width = tokens.shape
    top_count = routes.shape[1]
    experts = router_weight.shape[1]
    devices = lax.axis_size("ep")
    groups = devices // SHARD
    cols = 2
    planes = groups // cols
    ff = down_weight.shape[1]
    capacity = min(toks, SHARD * (17 * toks * top_count // (16 * experts * SHARD) + 1))
    wide = -(-(width + 2 * experts) // LANES) * LANES
    ffp = -(-ff // LANES) * LANES
    sect = planes * capacity
    count = planes * toks
    fan_in = cuts(wide, FAN_IN)
    fan_out = cuts(wide, FAN_OUT)
    n_in, n_out = len(fan_in), len(fan_out)
    wide_in, wide_out = wide_span(fan_in)[1], wide_span(fan_out)[1]
    most = max(fw for _, fw, _ in fan_out)
    spots = 2 * (planes - 1)
    bf16 = jnp.bfloat16
    vmem = pl.BlockSpec(memory_space=pltpu.VMEM)
    hbm = pl.BlockSpec(memory_space=pl.ANY)
    dma = lambda n: pltpu.SemaphoreType.DMA((2, n))
    return pl.pallas_call(
        functools.partial(moe_kernel, planes, cols, capacity, fan_in, fan_out),
        out_shape=jax.ShapeDtypeStruct((toks, width), bf16),
        in_specs=[vmem, vmem, vmem, vmem, hbm, hbm],
        out_specs=vmem,
        scratch_shapes=[
            pltpu.VMEM((2 * ffp, width), bf16),
            pltpu.VMEM((ff, width), bf16),
            pltpu.VMEM((ffp, wide), bf16),
            pltpu.VMEM((count, LANES), bf16),
            pltpu.VMEM((count, LANES), bf16),
            pltpu.VMEM((count, wide), bf16),
            pltpu.VMEM((count, wide_in), bf16),
            pltpu.VMEM((8 * sect, wide), bf16),
            pltpu.VMEM((2 * sect, wide), bf16),
            pltpu.VMEM((8 * sect, 2 * ffp), jnp.float32),
            pltpu.VMEM((8 * sect, ffp), bf16),
            pltpu.VMEM((8 * sect, wide), bf16),
            pltpu.VMEM((4 * sect, wide), bf16),
            pltpu.VMEM((2 * sect, wide), bf16),
            pltpu.VMEM((2 * sect, wide), bf16),
            pltpu.VMEM((2 * sect, wide_out), bf16),
            pltpu.VMEM((count, wide), bf16),
            pltpu.VMEM((count, wide_out), bf16),
            pltpu.VMEM((spots, toks, wide), bf16),
            pltpu.VMEM((spots, toks, wide_out), bf16),
            pltpu.VMEM((toks, most), jnp.float32),
            pltpu.VMEM((toks, wide_out), bf16),
            pltpu.VMEM((toks, wide_out), bf16),
            pltpu.SemaphoreType.DMA((3,)),
            dma(2 * planes - 1),
            dma(n_in),
            dma(n_in * 2 * spots),
            dma(2 * n_in),
            dma(2 * n_in),
            dma(4 * n_in),
            dma(4 * n_out),
            dma(2 * n_out),
            dma(2 * n_out),
            dma(n_out * 2 * spots),
            dma(n_out),
        ],
        compiler_params=pltpu.CompilerParams(
            collective_id=0, has_side_effects=True, vmem_limit_bytes=63 * 1024 * 1024
        ),
    )(
        tokens,
        routes.T,
        norm_gain,
        router_weight.T,
        gate_up_weight[0].T,
        down_weight[0],
    )


def solution(mesh):
    in_specs = (
        P(("groups", "ep"), None),
        P(("groups", "ep"), None),
        P(),
        P(),
        P("ep", None, None),
        P("ep", None, None),
    )
    out_specs = P(("groups", "ep"), None)
    return jax.shard_map(shards, mesh=mesh, in_specs=in_specs, out_specs=out_specs, check_vma=False)
```

time: 141 us -> 116 us (0.82)
  Pallas kernels: 128 us -> 114 us
  local copies, waits for them, and re-layouts: 12.9 us -> 1.76 us
    pallas_call x1, Pallas kernels: 128 us -> 114 us  [shards(): pl.pallas_call(functools.partial(moe_kernel, planes, cols, capacity, fan_...]
    unnamed x4 -> x1, local copies, waits for them, and re-layouts: 11.6 us -> 1.76 us
where the time goes in v2:
time: 116 us
  Pallas kernels  114 us (98%)
  local copies, waits for them, and re-layouts  1.76 us (2%)
    pallas_call x1, Pallas kernels, shards(): pl.pallas_call(functools.partial(moe_kernel, planes, cols, capacity, fan_...  114 us

profile of v2, /device:TPU:0, one launch (start us, length us, event | category | flops | bytes accessed | tf_op | source)
XLA Modules:
  0.0 115.7 jit_solution(1377351365578912031)
XLA Ops:
  0.0 113.9 %shard_map.64 = bf16[64,2880]{1,0:T(8,128)(2,1)} custom-call(bf16[64,2880]{1,0:T(8,128)(2,1)} %tokens.1, s32[4,64]{1,0:T(4,128)} %bitcast.9, bf16[2880]{0:T(1024)(128)(2,1)} %gain.1, bf16[8,2880]{1,0:T(8,128)(2,1)} %bitcast.8, bf16[720,2880]{1,0:T(8,128)(2,1)} %bitcast.6, bf16[360,2880]{1,0:T(8,128)(2,1)} %bitcast.7), custom_call_target="tpu_custom_call" | custom-call | tf_op jit(solution)/shard_map/pallas_call | solution.py:678
  113.9 1.8 %copy.8 = bf16[64,2880]{1,0:T(8,128)(2,1)} copy(bf16[64,2880]{1,0:T(8,128)(2,1)} %shard_map.64) | data formatting | bytes 737280
